TPU v7x, 32 devices: a whole 2x2x4 slice. The times are simulated.
32 devices in a mesh: ctx: 16 (over z, y, x), head: 2 (over core).
Axes of the slice: x: 2, y: 2, z: 4, core: 2. Of those that a mesh axis runs over, the one named last changes fastest.
Arguments:
- queries: bfloat16 [8192, 2048], P('ctx', 'head'), may hold values from -24 to 24
- keys: bfloat16 [8192, 2048], P('ctx', 'head'), may hold values from -24 to 24
- values: bfloat16 [8192, 2048], P('ctx', 'head'), may hold values from -6 to 6
- prefix_keys: bfloat16 [8192, 2048], P('ctx', 'head'), may hold values from -6 to 6
- prefix_values: bfloat16 [8192, 2048], P('ctx', 'head'), may hold values from -6 to 6
- selected: int32 [2, 64, 8, 3], P('head', 'ctx'), may hold values from 0 to 15, all different within a row; in each aligned block of 32 rows (0 to 31, 32 to 63, ..., all dimensions but the last counted through in order) at most 6 rows name the same one
- out_weight: bfloat16 [2, 1024, 4096], P('head', 'ctx'), may hold values from -0.125 to 0.125
Outputs:
- mixed: bfloat16 [8192, 4096], P('ctx', 'head')
Inputs may be any that keep to these rules, and one draw needn't show every extreme that they name: `selected`: for every head group, tile and head, 3 different prefix blocks. Among the 32 rows of one device (one head group, that device's tiles), no block is named more than 6 times.
All inputs are finite; a program needn't handle non-finite values.
Results may differ from a plain program's by a relative error of at most 0.0056.
Values may be sent and summed in bfloat16 or wider, within the bound.
No kernel may reach another device: no remote copies, remote signals or barrier semaphores. Data moves between devices by JAX's collectives and lax.ppermute only.
A program may use at most 128 MiB of HBM per device.

v0:
```python
import math

import jax
import jax.numpy as jnp
from jax import lax
from jax.experimental import pallas as pl
from jax.experimental.pallas import tpu as pltpu
from jax.sharding import PartitionSpec as P


D_HEAD = 128
TILE = 128
BLOCK = 512
TOPK = 3
UNROLL = 24
SCALE = D_HEAD ** (-0.5)
LOG2E = 1.4426950408889634
BF16 = jnp.bfloat16
F32 = jnp.float32


def round_up(n, m):
    return (n + m - 1) // m * m


def smem():
    return pl.BlockSpec(memory_space=pltpu.SMEM)


def route_queries(picked, queries, peers, parts, blocks_here):
    tok_rows, width = queries.shape
    heads = width // D_HEAD
    requests = picked.shape[0]
    slots = sum(parts)
    tails = [round_up(n, 16) for n in parts]
    steps = 4 if peers % 4 == 0 else 1
    per_step = peers // steps
    full = peers * slots == requests

    def body(picked_ref, q_ref, *refs):
        outs, (owner_ref, rank_ref, source, pair, count) = refs[: len(parts)], refs[len(parts) :]
        step = pl.program_id(0)

        @pl.when(step == 0)
        def _():
            for p in range(peers):
                count[p] = 0
            if not full:
                for i in range(peers * slots):
                    source[i] = -1
                    pair[i] = 0
            for r in range(requests):
                block = picked_ref[r]
                owner = block // blocks_here if blocks_here > 1 else block
                local = block % blocks_here if blocks_here > 1 else 0
                rank = count[owner]
                slot = owner * slots + rank
                source[slot] = r // TOPK
                pair[slot] = local * heads + (r // TOPK) % heads
                count[owner] = rank + 1
                owner_ref[r] = owner
                rank_ref[r] = rank

        for i in range(per_step):
            first = 0
            for n, tail, out_ref in zip(parts, tails, outs):
                sub = lax.broadcasted_iota(jnp.int32, (tail, TILE), 0)
                ids = jnp.zeros((tail, TILE), F32)
                for s in range(n):
                    slot = (step * per_step + i) * slots + first + s
                    row = source[slot]
                    safe = row if full else jnp.maximum(row, 0)
                    start = pl.multiple_of((safe // heads) * TILE, TILE)
                    lane = pl.multiple_of((safe % heads) * D_HEAD, D_HEAD)
                    q = q_ref[pl.ds(start, TILE), pl.ds(lane, D_HEAD)]
                    if not full:
                        q = jnp.where(row >= 0, q, jnp.zeros_like(q))
                    out_ref[i, s * TILE : (s + 1) * TILE, :] = q
                    ids = jnp.where(sub == s, pair[slot].astype(F32), ids)
                out_ref[i, n * TILE :, :] = ids.astype(BF16)
                first += n

    rows = [n * TILE + tail for n, tail in zip(parts, tails)]
    results = pl.pallas_call(
        body,
        grid=(steps,),
        in_specs=[smem(), pl.BlockSpec((tok_rows, width), lambda i: (0, 0))],
        out_specs=[pl.BlockSpec((per_step, n, TILE), lambda i: (i, 0, 0)) for n in rows]
        + [smem(), smem()],
        out_shape=[jax.ShapeDtypeStruct((peers, n, TILE), BF16) for n in rows]
        + [jax.ShapeDtypeStruct((requests,), jnp.int32)] * 2,
        scratch_shapes=[
            pltpu.SMEM((peers * slots,), jnp.int32),
            pltpu.SMEM((peers * slots,), jnp.int32),
            pltpu.SMEM((peers,), jnp.int32),
        ],
        name="route",
    )(picked, queries)
    return results[: len(parts)], results[-2], results[-1]


def soft(scores):
    top = jnp.max(scores, axis=0, keepdims=True)
    weights = jnp.exp2((scores - top) * (SCALE * LOG2E))
    total = jnp.sum(weights, axis=0, keepdims=True)
    return weights.astype(BF16), total, top * SCALE + jnp.log(total)


def dot_nt(a, b):
    return lax.dot_general(a, b, (((1,), (1,)), ((), ())), preferred_element_type=F32)


def attend_slots(pairs, incoming, keys, values_t, slots, heads):
    peers, rows, _ = incoming.shape
    tail = round_up(3 * slots, 16)
    out_rows = slots * TILE + tail
    blocks = keys.shape[0] // BLOCK
    group = math.gcd(peers, max(1, UNROLL // slots))

    def body(pair_ref, q_ref, k_ref, v_ref, out_ref):
        sub = lax.broadcasted_iota(jnp.int32, (tail, TILE), 0)
        for i in range(group):
            p = pl.program_id(0) * group + i
            logs = jnp.zeros((tail, TILE), F32)
            for s in range(slots):
                pair = pair_ref[p * slots + s]
                head = pair % heads if blocks > 1 else pair
                start = pl.multiple_of(pair // heads * BLOCK, BLOCK) if blocks > 1 else 0
                lane = pl.multiple_of(head * D_HEAD, D_HEAD)
                k = k_ref[pl.ds(start, BLOCK), pl.ds(lane, D_HEAD)]
                v = v_ref[pl.ds(lane, D_HEAD), pl.ds(start, BLOCK)]
                q = q_ref[i, s * TILE : (s + 1) * TILE, :]
                weights, total, lse = soft(dot_nt(k, q))
                out = jnp.dot(v, weights, preferred_element_type=F32) / total
                out_ref[i, s * TILE : (s + 1) * TILE, :] = out.astype(BF16)
                high = lse.astype(BF16).astype(F32)
                middle = (lse - high).astype(BF16).astype(F32)
                low = lse - high - middle
                logs = jnp.where(sub == 3 * s, high, logs)
                logs = jnp.where(sub == 3 * s + 1, middle, logs)
                logs = jnp.where(sub == 3 * s + 2, low, logs)
            out_ref[i, slots * TILE :, :] = logs.astype(BF16)

    return pl.pallas_call(
        body,
        grid=(peers // group,),
        in_specs=[
            smem(),
            pl.BlockSpec((group, rows, TILE), lambda i: (i, 0, 0)),
            pl.BlockSpec(keys.shape, lambda i: (0, 0)),
            pl.BlockSpec(values_t.shape, lambda i: (0, 0)),
        ],
        out_specs=pl.BlockSpec((group, out_rows, TILE), lambda i: (i, 0, 0)),
        out_shape=jax.ShapeDtypeStruct((peers, out_rows, TILE), BF16),
        name="attend",
    )(pairs, incoming, keys, values_t)


def own_attention(queries, keys, values, prefix_values):
    tok_rows, width = queries.shape
    heads = width // D_HEAD
    blocks = tok_rows // BLOCK

    def body(q_ref, k_ref, v_ref, pv_ref, out_ref, lse_ref, turned_ref):
        turned_ref[...] = pv_ref[...].T
        v_t = v_ref[...].T
        for t in range(BLOCK // TILE):
            seen = (t + 1) * TILE
            scores = dot_nt(k_ref[:seen, :], q_ref[t * TILE : seen, :])
            key = lax.broadcasted_iota(jnp.int32, scores.shape, 0)
            query = lax.broadcasted_iota(jnp.int32, scores.shape, 1) + t * TILE
            weights, total, lse = soft(jnp.where(key <= query, scores, -jnp.inf))
            out = jnp.dot(v_t[:, :seen], weights, preferred_element_type=F32) / total
            out_ref[:, t * TILE : seen] = out
            lse_ref[0, :, t * TILE : seen] = lse

    block = pl.BlockSpec((BLOCK, D_HEAD), lambda b, h: (b, h))
    block_t = pl.BlockSpec((D_HEAD, BLOCK), lambda b, h: (h, b))
    return pl.pallas_call(
        body,
        grid=(blocks, heads),
        in_specs=[block] * 4,
        out_specs=[block_t, pl.BlockSpec((1, 1, BLOCK), lambda b, h: (h, 0, b)), block_t],
        out_shape=[
            jax.ShapeDtypeStruct((width, tok_rows), F32),
            jax.ShapeDtypeStruct((heads, 1, tok_rows), F32),
            jax.ShapeDtypeStruct((width, tok_rows), BF16),
        ],
        name="own",
    )(queries, keys, values, prefix_values)


def combine(owner, rank, place, backs, own_out, own_lse, parts):
    peers = backs[0].shape[0]
    width, tok_rows = own_out.shape
    heads = width // D_HEAD
    tiles = tok_rows // TILE
    chunk = width // peers

    def body(owner_ref, rank_ref, place_ref, *refs):
        back_refs, (out_ref, lse_ref, att_ref, turned) = refs[: len(parts)], refs[len(parts) :]
        t = pl.program_id(0)

        def answer(r):
            p, rank = owner_ref[r], rank_ref[r]
            first, part, log = 0, None, None
            for n, back_ref in zip(parts, back_refs):
                s = jnp.clip(rank - first, 0, n - 1)
                here = back_ref[p, pl.ds(pl.multiple_of(s * TILE, TILE), TILE), :]
                terms = back_ref[p, n * TILE :, :].astype(F32)
                sub = lax.broadcasted_iota(jnp.int32, terms.shape, 0)
                mine = jnp.logical_and(sub >= 3 * s, sub < 3 * s + 3)
                here_log = jnp.sum(jnp.where(mine, terms, 0.0), axis=0, keepdims=True)
                part = here if part is None else jnp.where(rank >= first, here, part)
                log = here_log if log is None else jnp.where(rank >= first, here_log, log)
                first += n
            return part.astype(F32), log

        for h in range(heads):
            logs, pieces = [lse_ref[h]], [out_ref[h * D_HEAD : (h + 1) * D_HEAD, :]]
            for j in range(TOPK):
                piece, log = answer((t * heads + h) * TOPK + j)
                pieces.append(piece)
                logs.append(log)
            top = logs[0]
            for log in logs[1:]:
                top = jnp.maximum(top, log)
            factors = [jnp.exp(log - top) for log in logs]
            total = factors[0]
            for factor in factors[1:]:
                total = total + factor
            inverse = 1.0 / total
            mixed = pieces[0] * (factors[0] * inverse)
            for factor, piece in zip(factors[1:], pieces[1:]):
                mixed = mixed + piece * (factor * inverse)
            for i in range(D_HEAD // chunk):
                at = pl.multiple_of(place_ref[h * (D_HEAD // chunk) + i] * chunk, chunk)
                turned[pl.ds(at, chunk), :] = mixed[i * chunk : (i + 1) * chunk, :]
        for h in range(heads):
            lanes = slice(h * D_HEAD, (h + 1) * D_HEAD)
            att_ref[:, lanes] = turned[lanes, :].T.astype(BF16)

    return pl.pallas_call(
        body,
        grid=(tiles,),
        in_specs=[smem(), smem(), smem()]
        + [pl.BlockSpec(back.shape, lambda i: (0, 0, 0)) for back in backs]
        + [
            pl.BlockSpec((width, TILE), lambda i: (0, i)),
            pl.BlockSpec((heads, 1, TILE), lambda i: (0, 0, i)),
        ],
        out_specs=pl.BlockSpec((TILE, width), lambda i: (i, 0)),
        out_shape=jax.ShapeDtypeStruct((tok_rows, width), BF16),
        scratch_shapes=[pltpu.VMEM((width, TILE), F32)],
        name="combine",
    )(owner, rank, place, *backs, own_out, own_lse)


def project(att_own, att_other, halves):
    rows, depth = att_own.shape
    piece, columns = halves[0][0].shape
    part = min(columns, 1024)
    count = columns // part

    def body(a_ref, b_ref, *refs):
        out_ref = refs[-1]
        for i in range(len(halves)):
            w0, w1, w2, w3 = refs[4 * i : 4 * i + 4]

            @pl.when(pl.program_id(0) // count == i)
            def _():
                total = jnp.dot(a_ref[:, :piece], w0[...], preferred_element_type=F32)
                total += jnp.dot(a_ref[:, piece:], w1[...], preferred_element_type=F32)
                total += jnp.dot(b_ref[:, :piece], w2[...], preferred_element_type=F32)
                total += jnp.dot(b_ref[:, piece:], w3[...], preferred_element_type=F32)
                out_ref[...] = total.astype(BF16)

    def weight(i):
        return pl.BlockSpec((piece, part), lambda n: (0, jnp.clip(n - i * count, 0, count - 1)))

    held = pl.BlockSpec((rows, depth), lambda n: (0, 0))
    return pl.pallas_call(
        body,
        grid=(len(halves) * count,),
        in_specs=[held, held] + [weight(i) for i in range(len(halves)) for _ in range(4)],
        out_specs=pl.BlockSpec((rows, part), lambda n: (0, n)),
        out_shape=jax.ShapeDtypeStruct((rows, len(halves) * columns), BF16),
        name="project",
    )(att_own, att_other, *[w for half in halves for w in half])


def bit_orders(peers):
    bits = int(math.log2(peers))
    high = list(range(bits - 1, 2, -1))
    return [high + [2, 1, 0], high + [2, 0, 1]]


def doubling_pairs(peers, orders, step, crossed=False):
    pairs = []
    for c in range(peers):
        for h in range(2):
            pairs.append((2 * c + h, 2 * (c ^ (1 << orders[h][step])) + (1 - h if crossed else h)))
    return pairs


def joined(a, b):
    return lax.optimization_barrier(jnp.concatenate([a, b], axis=0))


def stacked_halves(pieces, core):
    rows, width = pieces[0].shape
    half, count = width // 2, len(pieces)
    step = rows // 4 if rows % 64 == 0 else rows

    def body(core_ref, *refs):
        mine_ref, theirs_ref = refs[2 * count :]
        for i in range(count):
            mine_ref[i], theirs_ref[i] = refs[i][...], refs[count + i][...]

    mine = pl.BlockSpec((step, half), lambda i, core_ref: (i, core_ref[0]))
    theirs = pl.BlockSpec((step, half), lambda i, core_ref: (i, 1 - core_ref[0]))
    out = pl.BlockSpec((count, step, half), lambda i, core_ref: (0, i, 0))
    results = pl.pallas_call(
        body,
        grid_spec=pltpu.PrefetchScalarGridSpec(
            num_scalar_prefetch=1,
            grid=(rows // step,),
            in_specs=[mine] * count + [theirs] * count,
            out_specs=[out, out],
        ),
        out_shape=[jax.ShapeDtypeStruct((count, rows, half), pieces[0].dtype)] * 2,
        name="halves",
    )(core.reshape(1), *pieces, *pieces)
    return [result.reshape(count * rows, half) for result in results]


def shards(queries, keys, values, prefix_keys, prefix_values, selected, out_weight):
    tok_rows, width = queries.shape
    heads = width // D_HEAD
    tiles = tok_rows // TILE
    blocks_here = prefix_keys.shape[0] // BLOCK
    peers = lax.axis_size("ctx")
    me, core = lax.axis_index("ctx"), lax.axis_index("head")
    requests = tiles * heads * TOPK
    capacity = -(-requests // (peers * blocks_here))
    slots = capacity * blocks_here
    swap = [(0, 1), (1, 0)]
    both = ("ctx", "head")

    orders = bit_orders(peers)
    steps = len(orders[0])

    def gathered(weight):
        for step in range(steps - 3):
            got = lax.ppermute(weight, both, doubling_pairs(peers, orders, step))
            weight = joined(weight, got)
        pieces = [weight]
        for step in range(steps - 3, steps - 1):
            pairs = doubling_pairs(peers, orders, step)
            pieces += [lax.ppermute(piece, both, pairs) for piece in pieces]
        mine, theirs = stacked_halves(pieces, core)
        far_own = lax.ppermute(mine, both, doubling_pairs(peers, orders, steps - 1))
        far_other = lax.ppermute(theirs, both, doubling_pairs(peers, orders, steps - 1, True))
        near_other = lax.ppermute(theirs, "head", swap)
        return mine, far_own, near_other, far_other

    weights = [gathered(out_weight[0])]

    parts = [slots]
    outgoing, owner, rank = route_queries(
        selected.reshape(requests), queries, peers, parts, blocks_here
    )
    incoming = []
    for sent in outgoing:
        incoming.append(lax.all_to_all(sent, "ctx", split_axis=0, concat_axis=0, tiled=True))
    own_out, own_lse, turned = own_attention(queries, keys, values, prefix_values)

    apart = jnp.arange(peers, dtype=jnp.int32) ^ me
    places = [sum(((apart >> bit) & 1) << k for k, bit in enumerate(order)) for order in orders]
    place = jnp.where(core == 0, places[0], places[1])

    backs = []
    for n, asked in zip(parts, incoming):
        pairs = asked[:, n * TILE : n * TILE + n, 0].astype(jnp.int32).reshape(peers * n)
        answers = attend_slots(pairs, asked, prefix_keys, turned, n, heads)
        backs.append(lax.all_to_all(answers, "ctx", split_axis=0, concat_axis=0, tiled=True))
    att = combine(owner, rank, place, backs, own_out, own_lse, parts)
    att_other = lax.ppermute(att, "head", swap)
    return project(att, att_other, weights)


def solution(mesh):
    return jax.shard_map(
        shards,
        mesh=mesh,
        in_specs=(
            P("ctx", "head"),
            P("ctx", "head"),
            P("ctx", "head"),
            P("ctx", "head"),
            P("ctx", "head"),
            P("head", "ctx", None, None),
            P("head", "ctx", None),
        ),
        out_specs=P("ctx", "head"),
        check_vma=False,
    )
```

profile of v0, /device:TPU:0, one launch (start us, length us, event | category | flops | bytes accessed | tf_op | source)
XLA Modules:
  0.0 306.6 jit_solution(12334992608865224141)
XLA Ops:
  0.0 0.8 copy.9
  0.8 0.6 reshape.16.picked_ref
  1.4 4.4 %route.1 = (bf16[16,784,128]{2,1,0:T(8,128)(2,1)}, s32[96]{0:T(128)}, s32[96]{0:T(128)}) custom-call(s32[96]{0:T(128)} %reshape.16.picked_ref, bf16[512,1024]{1,0:T(8,128)(2,1)} %q_ref.3), custom_call_target="tpu_custom_call" | custom-call | tf_op jit(solution)/shard_map/route/pallas_call | solution.py:84
  5.8 8.3 %all-to-all-start = ((bf16[16,784,128]{2,1,0:T(8,128)(2,1)}), bf16[16,784,128]{2,1,0:T(8,128)(2,1)S(1)}, u32[]{:S(2)}, u32[]{:S(2)}) async-start(bf16[16,784,128]{2,1,0:T(8,128)(2,1)} %get-tuple-element.15), calls=%async_computation | async-start | bytes 6422528 | tf_op jit(solution)/shard_map/all_to_all | solution.py:375
  14.1 10.2 %own.1 = (f32[1024,512]{1,0:T(8,128)}, f32[8,1,512]{2,1,0:T(1,128)}, bf16[1024,512]{1,0:T(8,128)(2,1)}) custom-call(bf16[512,1024]{1,0:T(8,128)(2,1)} %q_ref.3, bf16[512,1024]{1,0:T(8,128)(2,1)} %k_ref.2, bf16[512,1024]{1,0:T(8,128)(2,1)} %v_ref.1, bf16[512,1024]{1,0:T(8,128)(2,1)} %pv_ref.1), custom_call_target="tpu_custom_call" | custom-call | tf_op jit(solution)/shard_map/own/pallas_call | solution.py:179
  24.4 51.8 %all-to-all-done.q_ref = bf16[16,784,128]{2,1,0:T(8,128)(2,1)S(1)} async-done(((bf16[16,784,128]{2,1,0:T(8,128)(2,1)}), bf16[16,784,128]{2,1,0:T(8,128)(2,1)S(1)}, u32[]{:S(2)}, u32[]{:S(2)}) %all-to-all-start) | async-done | bytes 3211296 | tf_op jit(solution)/shard_map/all_to_all | solution.py:375
  76.1 0.3 convert_reduce_fusion
  76.5 1.0 reshape.20.pair_ref
  77.5 0.3 copy-done.1
  77.8 13.9 %attend.1 = bf16[16,800,128]{2,1,0:T(8,128)(2,1)} custom-call(s32[96]{0:T(128)} %reshape.20.pair_ref, bf16[16,784,128]{2,1,0:T(8,128)(2,1)} %copy-done.1, bf16[512,1024]{1,0:T(8,128)(2,1)} %k_ref.3, bf16[1024,512]{1,0:T(8,128)(2,1)} %get-tuple-element.16.v_ref), custom_call_target="tpu_custom_call" | custom-call | tf_op jit(solution)/shard_map/attend/pallas_call | solution.py:144
  91.8 15.4 %all-to-all-start.1 = ((bf16[16,800,128]{2,1,0:T(8,128)(2,1)}), bf16[16,800,128]{2,1,0:T(8,128)(2,1)S(1)}, u32[]{:S(2)}, u32[]{:S(2)}) async-start(bf16[16,800,128]{2,1,0:T(8,128)(2,1)} %attend.1), calls=%async_computation.1 | async-start | bytes 6553600 | tf_op jit(solution)/shard_map/all_to_all | solution.py:386
  107.2 2.8 collective-permute-start.1
  110.0 92.4 %collective-permute-done.1 = bf16[64,4096]{1,0:T(8,128)(2,1)S(1)} collective-permute-done((bf16[64,4096]{1,0:T(8,128)(2,1)}, bf16[64,4096]{1,0:T(8,128)(2,1)S(1)}, u32[]{:S(2)}, u32[]{:S(2)}) %collective-permute-start.1) | collective-permute-done | bytes 524320 | tf_op jit(solution)/shard_map/ppermute | solution.py:355
  202.5 2.2 pad_maximum_fusion.refs_0_.refs_4_
  204.7 0.0 collective-permute-start.2
  204.7 2.5 collective-permute-start.3
  207.2 22.0 %collective-permute-done.2.refs_1_.refs_5_ = bf16[128,4096]{1,0:T(8,128)(2,1)} collective-permute-done((bf16[128,4096]{1,0:T(8,128)(2,1)}, bf16[128,4096]{1,0:T(8,128)(2,1)}, u32[]{:S(2)}, u32[]{:S(2)}) %collective-permute-start.2) | collective-permute-done | bytes 1048608 | tf_op jit(solution)/shard_map/ppermute | solution.py:360
  229.2 2.5 collective-permute-start.4
  231.7 13.1 %collective-permute-done.4.refs_3_.refs_7_ = bf16[128,4096]{1,0:T(8,128)(2,1)} collective-permute-done((bf16[128,4096]{1,0:T(8,128)(2,1)}, bf16[128,4096]{1,0:T(8,128)(2,1)}, u32[]{:S(2)}, u32[]{:S(2)}) %collective-permute-start.4) | collective-permute-done | bytes 1048608 | tf_op jit(solution)/shard_map/ppermute | solution.py:360
  244.8 4.8 %halves.1 = (bf16[4,128,2048]{2,1,0:T(8,128)(2,1)}, bf16[4,128,2048]{2,1,0:T(8,128)(2,1)}) custom-call(s32[1]{0:T(128)} %bitcast.core_ref, bf16[128,4096]{1,0:T(8,128)(2,1)} %pad_maximum_fusion.refs_0_.refs_4_, bf16[128,4096]{1,0:T(8,128)(2,1)} %collective-permute-done.2.refs_1_.refs_5_, bf16[128,4096]{1,0:T(8,128)(2,1)} %collective-permute-done.3.refs_2_.refs_6_, ...), custom_call_target="tpu_custom_call" | custom-call | tf_op jit(solution)/shard_map/halves/pallas_call | solution.py:323
  249.5 1.0 collective-permute-start.5
  250.5 0.0 collective-permute-start.6
  250.5 1.2 collective-permute-start.7
  251.7 0.5 broadcast_select_fusion.place_ref
  252.2 0.0 all-to-all-done.1.refs_0_
  252.2 1.7 copy-done
  253.9 5.7 %combine.1.a_ref = bf16[512,1024]{1,0:T(8,128)(2,1)} custom-call(s32[96]{0:T(128)} %get-tuple-element.13.owner_ref, s32[96]{0:T(128)} %get-tuple-element.14.rank_ref, s32[16]{0:T(128)} %broadcast_select_fusion.place_ref, bf16[16,800,128]{2,1,0:T(8,128)(2,1)} %copy-done, f32[1024,512]{1,0:T(8,128)} %get-tuple-element.17.refs_1_, ...), custom_call_target="tpu_custom_call" | custom-call | tf_op jit(solution)/shard_map/combine/pallas_call | solution.py:243
  259.6 0.5 collective-permute-start
  260.0 15.8 %collective-permute-done.5.refs_1_ = bf16[512,2048]{1,0:T(8,128)(2,1)} collective-permute-done((bf16[512,2048]{1,0:T(8,128)(2,1)}, bf16[512,2048]{1,0:T(8,128)(2,1)}, u32[]{:S(2)}, u32[]{:S(2)}) %collective-permute-start.5) | collective-permute-done | bytes 2097184 | tf_op jit(solution)/shard_map/ppermute | solution.py:362
  275.9 21.0 %collective-permute-done.7.refs_3_ = bf16[512,2048]{1,0:T(8,128)(2,1)} collective-permute-done((bf16[512,2048]{1,0:T(8,128)(2,1)}, bf16[512,2048]{1,0:T(8,128)(2,1)}, u32[]{:S(2)}, u32[]{:S(2)}) %collective-permute-start.7) | collective-permute-done | bytes 2097184 | tf_op jit(solution)/shard_map/ppermute | solution.py:363
  296.9 1.0 copy-done.2
  297.8 8.8 %project.1 = bf16[512,2048]{1,0:T(8,128)(2,1)} custom-call(bf16[512,1024]{1,0:T(8,128)(2,1)} %combine.1.a_ref, bf16[512,1024]{1,0:T(8,128)(2,1)} %copy-done.2, bf16[512,2048]{1,0:T(8,128)(2,1)} %bitcast.7, bf16[512,2048]{1,0:T(8,128)(2,1)} %collective-permute-done.5.refs_1_, bf16[512,2048]{1,0:T(8,128)(2,1)} %collective-permute-done.6.refs_2_, ...), custom_call_target="tpu_custom_call" | custom-call | tf_op jit(solution)/shard_map/project/pallas_call | solution.py:282
  (6 shorter events, 0.0 us)
Async XLA Ops:
  5.8 70.4 %all-to-all-start = ((bf16[16,784,128]{2,1,0:T(8,128)(2,1)}), bf16[16,784,128]{2,1,0:T(8,128)(2,1)S(1)}, u32[]{:S(2)}, u32[]{:S(2)}) async-start(bf16[16,784,128]{2,1,0:T(8,128)(2,1)} %get-tuple-element.15), calls=%async_computation | async-start | bytes 6422528 | tf_op jit(solution)/shard_map/all_to_all | solution.py:375
  76.1 1.7 copy-start.1
  91.8 160.5 %all-to-all-start.1 = ((bf16[16,800,128]{2,1,0:T(8,128)(2,1)}), bf16[16,800,128]{2,1,0:T(8,128)(2,1)S(1)}, u32[]{:S(2)}, u32[]{:S(2)}) async-start(bf16[16,800,128]{2,1,0:T(8,128)(2,1)} %attend.1), calls=%async_computation.1 | async-start | bytes 6553600 | tf_op jit(solution)/shard_map/all_to_all | solution.py:386
  107.2 95.2 %collective-permute-start.1 = (bf16[64,4096]{1,0:T(8,128)(2,1)}, bf16[64,4096]{1,0:T(8,128)(2,1)S(1)}, u32[]{:S(2)}, u32[]{:S(2)}) collective-permute-start(bf16[64,4096]{1,0:T(8,128)(2,1)} %bitcast.8), channel_id=1, source_target_pairs={{0,16},{1,17},{2,18},{3,19},{4,20},{5,21},{6,22},{7,23},{8,24},{9,... | collective-permute-start | bytes 1572872 | tf_op jit(solution)/shard_map/ppermute | solution.py:355
  204.7 24.5 %collective-permute-start.2 = (bf16[128,4096]{1,0:T(8,128)(2,1)}, bf16[128,4096]{1,0:T(8,128)(2,1)}, u32[]{:S(2)}, u32[]{:S(2)}) collective-permute-start(bf16[128,4096]{1,0:T(8,128)(2,1)} %pad_maximum_fusion.refs_0_.refs_4_), channel_id=1, source_target_pairs={{0,8},{1,9},{2,10},{3,11},{4,12},{5,13},{6,14},{7,15},{8,0},{9,1},... | collective-permute-start | bytes 3145736 | tf_op jit(solution)/shard_map/ppermute | solution.py:360
  204.7 27.0 %collective-permute-start.3 = (bf16[128,4096]{1,0:T(8,128)(2,1)}, bf16[128,4096]{1,0:T(8,128)(2,1)}, u32[]{:S(2)}, u32[]{:S(2)}) collective-permute-start(bf16[128,4096]{1,0:T(8,128)(2,1)} %pad_maximum_fusion.refs_0_.refs_4_), channel_id=1, source_target_pairs={{0,4},{1,3},{2,6},{3,1},{4,0},{5,7},{6,2},{7,5},{8,12},{9,11},{10,... | collective-permute-start | bytes 3145736 | tf_op jit(solution)/shard_map/ppermute | solution.py:360
  229.2 15.6 %collective-permute-start.4 = (bf16[128,4096]{1,0:T(8,128)(2,1)}, bf16[128,4096]{1,0:T(8,128)(2,1)}, u32[]{:S(2)}, u32[]{:S(2)}) collective-permute-start(bf16[128,4096]{1,0:T(8,128)(2,1)} %collective-permute-done.2.refs_1_.refs_5_), channel_id=1, source_target_pairs={{0,4},{1,3},{2,6},{3,1},{4,0},{5,7},{6,2},{7,5},{8,12},{9,11},{10,... | collective-permute-start | bytes 3145736 | tf_op jit(solution)/shard_map/ppermute | solution.py:360
  249.5 26.4 %collective-permute-start.5 = (bf16[512,2048]{1,0:T(8,128)(2,1)}, bf16[512,2048]{1,0:T(8,128)(2,1)}, u32[]{:S(2)}, u32[]{:S(2)}) collective-permute-start(bf16[512,2048]{1,0:T(8,128)(2,1)} %bitcast.6), channel_id=1, source_target_pairs={{0,2},{1,5},{2,0},{3,7},{4,6},{5,1},{6,4},{7,3},{8,10},{9,13},{10,... | collective-permute-start | bytes 6291464 | tf_op jit(solution)/shard_map/ppermute | solution.py:362
  250.5 25.4 %collective-permute-start.6 = (bf16[512,2048]{1,0:T(8,128)(2,1)}, bf16[512,2048]{1,0:T(8,128)(2,1)}, u32[]{:S(2)}, u32[]{:S(2)}) collective-permute-start(bf16[512,2048]{1,0:T(8,128)(2,1)} %bitcast.10), channel_id=1, source_target_pairs={{0,1},{1,0},{2,3},{3,2},{4,5},{5,4},{6,7},{7,6},{8,9},{9,8},{10,11... | collective-permute-start | bytes 6291464 | tf_op jit(solution)/shard_map/ppermute | solution.py:364
  250.5 46.3 %collective-permute-start.7 = (bf16[512,2048]{1,0:T(8,128)(2,1)}, bf16[512,2048]{1,0:T(8,128)(2,1)}, u32[]{:S(2)}, u32[]{:S(2)}) collective-permute-start(bf16[512,2048]{1,0:T(8,128)(2,1)} %bitcast.11), channel_id=1, source_target_pairs={{0,3},{1,4},{2,1},{3,6},{4,7},{5,0},{6,5},{7,2},{8,11},{9,12},{10,... | collective-permute-start | bytes 6291464 | tf_op jit(solution)/shard_map/ppermute | solution.py:363
  252.2 1.7 copy-start
  259.6 37.3 %collective-permute-start = (bf16[512,1024]{1,0:T(8,128)(2,1)}, bf16[512,1024]{1,0:T(8,128)(2,1)S(1)}, u32[]{:S(2)}, u32[]{:S(2)}) collective-permute-start(bf16[512,1024]{1,0:T(8,128)(2,1)} %combine.1.a_ref), channel_id=1, source_target_pairs={{0,1},{1,0},{2,3},{3,2},{4,5},{5,4},{6,7},{7,6},{8,9},{9,8},{10,11... | collective-permute-start | bytes 3145736 | tf_op jit(solution)/shard_map/ppermute | solution.py:388
  296.8 1.0 copy-start.2
where the time goes:
time: 308 us; the launch traced here: 307 us
  waiting for transfers between devices  216 us (70%)
  Pallas kernels  47.8 us (16%)
  starting transfers between devices  34.2 us (11%)
  local copies, waits for them, and re-layouts  5.42 us (2%)
  other arithmetic  3.08 us (1%)
    ppermute x1, waiting for transfers between devices, gathered(): got = lax.ppermute(weight, both, doubling_pairs(peers, orders, step))  92.4 us
    all_to_all x1, waiting for transfers between devices, shards(): lax.all_to_all(sent, 'ctx', split_axis=0, concat_axis=0, tiled=True)  51.8 us
    ppermute x3, waiting for transfers between devices, gathered(): pieces += [lax.ppermute(piece, both, pairs) for piece in pieces]  35.1 us
    ppermute x1, waiting for transfers between devices, gathered(): lax.ppermute(theirs, both, doubling_pairs(peers, orders, steps - 1, True))  21 us
    ppermute x1, waiting for transfers between devices, gathered(): far_own = lax.ppermute(mine, both, doubling_pairs(peers, orders, steps - 1))  15.8 us
    all_to_all x1, starting transfers between devices, shards(): lax.all_to_all(answers, 'ctx', split_axis=0, concat_axis=0, tiled=True)  15.4 us
    pallas_call x1, Pallas kernels, attend_slots(): pl.pallas_call(body, grid=(peers // group,), in_specs=[smem(), pl.BlockSp...  13.9 us
    pallas_call x1, Pallas kernels, own_attention(): pl.pallas_call(body, grid=(blocks, heads), in_specs=[block] * 4, out_spec...  10.2 us
  transfers between devices with their start and end apart: 10, of which 6 were waited for; matrix products, arithmetic and copies ran while one was open for 1% of the time, Pallas kernels for 7%

commit v1 on v0

--- a/solution.py
+++ b/solution.py
@@ -12,7 +12,7 @@
 TILE = 128
 BLOCK = 512
 TOPK = 3
-UNROLL = 24
+UNROLL = 48
 SCALE = D_HEAD ** (-0.5)
 LOG2E = 1.4426950408889634
 BF16 = jnp.bfloat16
@@ -33,7 +33,7 @@
     requests = picked.shape[0]
     slots = sum(parts)
     tails = [round_up(n, 16) for n in parts]
-    steps = 4 if peers % 4 == 0 else 1
+    steps = math.gcd(peers, 2)
     per_step = peers // steps
     full = peers * slots == requests
 
@@ -196,10 +196,10 @@
     heads = width // D_HEAD
     tiles = tok_rows // TILE
     chunk = width // peers
+    group = math.gcd(tiles, 2)
 
     def body(owner_ref, rank_ref, place_ref, *refs):
         back_refs, (out_ref, lse_ref, att_ref, turned) = refs[: len(parts)], refs[len(parts) :]
-        t = pl.program_id(0)
 
         def answer(r):
             p, rank = owner_ref[r], rank_ref[r]
@@ -216,42 +216,46 @@
                 first += n
             return part.astype(F32), log
 
-        for h in range(heads):
-            logs, pieces = [lse_ref[h]], [out_ref[h * D_HEAD : (h + 1) * D_HEAD, :]]
-            for j in range(TOPK):
-                piece, log = answer((t * heads + h) * TOPK + j)
-                pieces.append(piece)
-                logs.append(log)
-            top = logs[0]
-            for log in logs[1:]:
-                top = jnp.maximum(top, log)
-            factors = [jnp.exp(log - top) for log in logs]
-            total = factors[0]
-            for factor in factors[1:]:
-                total = total + factor
-            inverse = 1.0 / total
-            mixed = pieces[0] * (factors[0] * inverse)
-            for factor, piece in zip(factors[1:], pieces[1:]):
-                mixed = mixed + piece * (factor * inverse)
-            for i in range(D_HEAD // chunk):
-                at = pl.multiple_of(place_ref[h * (D_HEAD // chunk) + i] * chunk, chunk)
-                turned[pl.ds(at, chunk), :] = mixed[i * chunk : (i + 1) * chunk, :]
-        for h in range(heads):
-            lanes = slice(h * D_HEAD, (h + 1) * D_HEAD)
-            att_ref[:, lanes] = turned[lanes, :].T.astype(BF16)
+        for i in range(group):
+            t = pl.program_id(0) * group + i
+            cols = slice(i * TILE, (i + 1) * TILE)
+            for h in range(heads):
+                logs = [lse_ref[h, :, cols]]
+                pieces = [out_ref[h * D_HEAD : (h + 1) * D_HEAD, cols]]
+                for j in range(TOPK):
+                    piece, log = answer((t * heads + h) * TOPK + j)
+                    pieces.append(piece)
+                    logs.append(log)
+                top = logs[0]
+                for log in logs[1:]:
+                    top = jnp.maximum(top, log)
+                factors = [jnp.exp(log - top) for log in logs]
+                total = factors[0]
+                for factor in factors[1:]:
+                    total = total + factor
+                inverse = 1.0 / total
+                mixed = pieces[0] * (factors[0] * inverse)
+                for factor, piece in zip(factors[1:], pieces[1:]):
+                    mixed = mixed + piece * (factor * inverse)
+                for c in range(D_HEAD // chunk):
+                    at = pl.multiple_of(place_ref[h * (D_HEAD // chunk) + c] * chunk, chunk)
+                    turned[pl.ds(at, chunk), cols] = mixed[c * chunk : (c + 1) * chunk, :]
+            for h in range(heads):
+                lanes = slice(h * D_HEAD, (h + 1) * D_HEAD)
+                att_ref[cols, lanes] = turned[lanes, cols].T.astype(BF16)
 
     return pl.pallas_call(
         body,
-        grid=(tiles,),
+        grid=(tiles // group,),
         in_specs=[smem(), smem(), smem()]
         + [pl.BlockSpec(back.shape, lambda i: (0, 0, 0)) for back in backs]
         + [
-            pl.BlockSpec((width, TILE), lambda i: (0, i)),
-            pl.BlockSpec((heads, 1, TILE), lambda i: (0, 0, i)),
+            pl.BlockSpec((width, group * TILE), lambda i: (0, i)),
+            pl.BlockSpec((heads, 1, group * TILE), lambda i: (0, 0, i)),
         ],
-        out_specs=pl.BlockSpec((TILE, width), lambda i: (i, 0)),
+        out_specs=pl.BlockSpec((group * TILE, width), lambda i: (i, 0)),
         out_shape=jax.ShapeDtypeStruct((tok_rows, width), BF16),
-        scratch_shapes=[pltpu.VMEM((width, TILE), F32)],
+        scratch_shapes=[pltpu.VMEM((width, group * TILE), F32)],
         name="combine",
     )(owner, rank, place, *backs, own_out, own_lse)
 

time: 308 us -> 307 us (level)
  no operation moved by 1% of the time
where the time goes in v1:
time: 307 us; the launch traced here: 306 us
  waiting for transfers between devices  217 us (71%)
  Pallas kernels  46.3 us (15%)
  starting transfers between devices  34.2 us (11%)
  local copies, waits for them, and re-layouts  5.42 us (2%)
  other arithmetic  3.08 us (1%)
    ppermute x1, waiting for transfers between devices, gathered(): got = lax.ppermute(weight, both, doubling_pairs(peers, orders, step))  92.5 us
    all_to_all x1, waiting for transfers between devices, shards(): lax.all_to_all(sent, 'ctx', split_axis=0, concat_axis=0, tiled=True)  51.8 us
    ppermute x3, waiting for transfers between devices, gathered(): pieces += [lax.ppermute(piece, both, pairs) for piece in pieces]  35.1 us
    ppermute x1, waiting for transfers between devices, gathered(): lax.ppermute(theirs, both, doubling_pairs(peers, orders, steps - 1, True))  21 us
    ppermute x1, waiting for transfers between devices, gathered(): far_own = lax.ppermute(mine, both, doubling_pairs(peers, orders, steps - 1))  16.5 us
    all_to_all x1, starting transfers between devices, shards(): lax.all_to_all(answers, 'ctx', split_axis=0, concat_axis=0, tiled=True)  15.4 us
    pallas_call x1, Pallas kernels, attend_slots(): pl.pallas_call(body, grid=(peers // group,), in_specs=[smem(), pl.BlockSp...  13.6 us
    pallas_call x1, Pallas kernels, own_attention(): pl.pallas_call(body, grid=(blocks, heads), in_specs=[block] * 4, out_spec...  10.2 us
  transfers between devices with their start and end apart: 10, of which 6 were waited for; matrix products, arithmetic and copies ran while one was open for 1% of the time, Pallas kernels for 7%

profile of v1, /device:TPU:0, one launch (start us, length us, event | category | flops | bytes accessed | tf_op | source)
XLA Modules:
  0.0 305.8 jit_solution(6377930728413917054)
XLA Ops:
  0.0 0.8 copy.9
  0.8 0.6 reshape.16.picked_ref
  1.4 3.9 %route.1 = (bf16[16,784,128]{2,1,0:T(8,128)(2,1)}, s32[96]{0:T(128)}, s32[96]{0:T(128)}) custom-call(s32[96]{0:T(128)} %reshape.16.picked_ref, bf16[512,1024]{1,0:T(8,128)(2,1)} %q_ref.3), custom_call_target="tpu_custom_call" | custom-call | tf_op jit(solution)/shard_map/route/pallas_call | solution.py:84
  5.3 8.3 %all-to-all-start = ((bf16[16,784,128]{2,1,0:T(8,128)(2,1)}), bf16[16,784,128]{2,1,0:T(8,128)(2,1)S(1)}, u32[]{:S(2)}, u32[]{:S(2)}) async-start(bf16[16,784,128]{2,1,0:T(8,128)(2,1)} %get-tuple-element.15), calls=%async_computation | async-start | bytes 6422528 | tf_op jit(solution)/shard_map/all_to_all | solution.py:379
  13.7 10.2 %own.1 = (f32[1024,512]{1,0:T(8,128)}, f32[8,1,512]{2,1,0:T(1,128)}, bf16[1024,512]{1,0:T(8,128)(2,1)}) custom-call(bf16[512,1024]{1,0:T(8,128)(2,1)} %q_ref.3, bf16[512,1024]{1,0:T(8,128)(2,1)} %k_ref.2, bf16[512,1024]{1,0:T(8,128)(2,1)} %v_ref.1, bf16[512,1024]{1,0:T(8,128)(2,1)} %pv_ref.1), custom_call_target="tpu_custom_call" | custom-call | tf_op jit(solution)/shard_map/own/pallas_call | solution.py:179
  23.9 51.8 %all-to-all-done.q_ref = bf16[16,784,128]{2,1,0:T(8,128)(2,1)S(1)} async-done(((bf16[16,784,128]{2,1,0:T(8,128)(2,1)}), bf16[16,784,128]{2,1,0:T(8,128)(2,1)S(1)}, u32[]{:S(2)}, u32[]{:S(2)}) %all-to-all-start) | async-done | bytes 3211296 | tf_op jit(solution)/shard_map/all_to_all | solution.py:379
  75.7 0.3 convert_reduce_fusion
  76.0 1.0 reshape.20.pair_ref
  77.1 0.3 copy-done.1
  77.4 13.6 %attend.1 = bf16[16,800,128]{2,1,0:T(8,128)(2,1)} custom-call(s32[96]{0:T(128)} %reshape.20.pair_ref, bf16[16,784,128]{2,1,0:T(8,128)(2,1)} %copy-done.1, bf16[512,1024]{1,0:T(8,128)(2,1)} %k_ref.3, bf16[1024,512]{1,0:T(8,128)(2,1)} %get-tuple-element.16.v_ref), custom_call_target="tpu_custom_call" | custom-call | tf_op jit(solution)/shard_map/attend/pallas_call | solution.py:144
  91.0 15.4 %all-to-all-start.1 = ((bf16[16,800,128]{2,1,0:T(8,128)(2,1)}), bf16[16,800,128]{2,1,0:T(8,128)(2,1)S(1)}, u32[]{:S(2)}, u32[]{:S(2)}) async-start(bf16[16,800,128]{2,1,0:T(8,128)(2,1)} %attend.1), calls=%async_computation.1 | async-start | bytes 6553600 | tf_op jit(solution)/shard_map/all_to_all | solution.py:390
  106.4 2.8 collective-permute-start.1
  109.2 92.5 %collective-permute-done.1 = bf16[64,4096]{1,0:T(8,128)(2,1)S(1)} collective-permute-done((bf16[64,4096]{1,0:T(8,128)(2,1)}, bf16[64,4096]{1,0:T(8,128)(2,1)S(1)}, u32[]{:S(2)}, u32[]{:S(2)}) %collective-permute-start.1) | collective-permute-done | bytes 524320 | tf_op jit(solution)/shard_map/ppermute | solution.py:359
  201.7 2.2 pad_maximum_fusion.refs_0_.refs_4_
  203.9 0.0 collective-permute-start.2
  203.9 2.5 collective-permute-start.3
  206.4 22.0 %collective-permute-done.2.refs_1_.refs_5_ = bf16[128,4096]{1,0:T(8,128)(2,1)} collective-permute-done((bf16[128,4096]{1,0:T(8,128)(2,1)}, bf16[128,4096]{1,0:T(8,128)(2,1)}, u32[]{:S(2)}, u32[]{:S(2)}) %collective-permute-start.2) | collective-permute-done | bytes 1048608 | tf_op jit(solution)/shard_map/ppermute | solution.py:364
  228.4 2.5 collective-permute-start.4
  230.9 13.1 %collective-permute-done.4.refs_3_.refs_7_ = bf16[128,4096]{1,0:T(8,128)(2,1)} collective-permute-done((bf16[128,4096]{1,0:T(8,128)(2,1)}, bf16[128,4096]{1,0:T(8,128)(2,1)}, u32[]{:S(2)}, u32[]{:S(2)}) %collective-permute-start.4) | collective-permute-done | bytes 1048608 | tf_op jit(solution)/shard_map/ppermute | solution.py:364
  244.0 4.8 %halves.1 = (bf16[4,128,2048]{2,1,0:T(8,128)(2,1)}, bf16[4,128,2048]{2,1,0:T(8,128)(2,1)}) custom-call(s32[1]{0:T(128)} %bitcast.core_ref, bf16[128,4096]{1,0:T(8,128)(2,1)} %pad_maximum_fusion.refs_0_.refs_4_, bf16[128,4096]{1,0:T(8,128)(2,1)} %collective-permute-done.2.refs_1_.refs_5_, bf16[128,4096]{1,0:T(8,128)(2,1)} %collective-permute-done.3.refs_2_.refs_6_, ...), custom_call_target="tpu_custom_call" | custom-call | tf_op jit(solution)/shard_map/halves/pallas_call | solution.py:327
  248.7 1.0 collective-permute-start.5
  249.7 0.0 collective-permute-start.6
  249.7 1.2 collective-permute-start.7
  250.9 0.5 broadcast_select_fusion.place_ref
  251.4 0.0 all-to-all-done.1.refs_0_
  251.4 1.7 copy-done
  253.1 5.0 %combine.1.a_ref = bf16[512,1024]{1,0:T(8,128)(2,1)} custom-call(s32[96]{0:T(128)} %get-tuple-element.13.owner_ref, s32[96]{0:T(128)} %get-tuple-element.14.rank_ref, s32[16]{0:T(128)} %broadcast_select_fusion.place_ref, bf16[16,800,128]{2,1,0:T(8,128)(2,1)} %copy-done, f32[1024,512]{1,0:T(8,128)} %get-tuple-element.17.refs_1_, ...), custom_call_target="tpu_custom_call" | custom-call | tf_op jit(solution)/shard_map/combine/pallas_call | solution.py:247
  258.1 0.5 collective-permute-start
  258.6 16.5 %collective-permute-done.5.refs_1_ = bf16[512,2048]{1,0:T(8,128)(2,1)} collective-permute-done((bf16[512,2048]{1,0:T(8,128)(2,1)}, bf16[512,2048]{1,0:T(8,128)(2,1)}, u32[]{:S(2)}, u32[]{:S(2)}) %collective-permute-start.5) | collective-permute-done | bytes 2097184 | tf_op jit(solution)/shard_map/ppermute | solution.py:366
  275.1 21.0 %collective-permute-done.7.refs_3_ = bf16[512,2048]{1,0:T(8,128)(2,1)} collective-permute-done((bf16[512,2048]{1,0:T(8,128)(2,1)}, bf16[512,2048]{1,0:T(8,128)(2,1)}, u32[]{:S(2)}, u32[]{:S(2)}) %collective-permute-start.7) | collective-permute-done | bytes 2097184 | tf_op jit(solution)/shard_map/ppermute | solution.py:367
  296.1 1.0 copy-done.2
  297.0 8.8 %project.1 = bf16[512,2048]{1,0:T(8,128)(2,1)} custom-call(bf16[512,1024]{1,0:T(8,128)(2,1)} %combine.1.a_ref, bf16[512,1024]{1,0:T(8,128)(2,1)} %copy-done.2, bf16[512,2048]{1,0:T(8,128)(2,1)} %bitcast.7, bf16[512,2048]{1,0:T(8,128)(2,1)} %collective-permute-done.5.refs_1_, bf16[512,2048]{1,0:T(8,128)(2,1)} %collective-permute-done.6.refs_2_, ...), custom_call_target="tpu_custom_call" | custom-call | tf_op jit(solution)/shard_map/project/pallas_call | solution.py:286
  (6 shorter events, 0.0 us)
Async XLA Ops:
  5.3 70.4 %all-to-all-start = ((bf16[16,784,128]{2,1,0:T(8,128)(2,1)}), bf16[16,784,128]{2,1,0:T(8,128)(2,1)S(1)}, u32[]{:S(2)}, u32[]{:S(2)}) async-start(bf16[16,784,128]{2,1,0:T(8,128)(2,1)} %get-tuple-element.15), calls=%async_computation | async-start | bytes 6422528 | tf_op jit(solution)/shard_map/all_to_all | solution.py:379
  75.7 1.7 copy-start.1
  91.0 160.5 %all-to-all-start.1 = ((bf16[16,800,128]{2,1,0:T(8,128)(2,1)}), bf16[16,800,128]{2,1,0:T(8,128)(2,1)S(1)}, u32[]{:S(2)}, u32[]{:S(2)}) async-start(bf16[16,800,128]{2,1,0:T(8,128)(2,1)} %attend.1), calls=%async_computation.1 | async-start | bytes 6553600 | tf_op jit(solution)/shard_map/all_to_all | solution.py:390
  106.4 95.3 %collective-permute-start.1 = (bf16[64,4096]{1,0:T(8,128)(2,1)}, bf16[64,4096]{1,0:T(8,128)(2,1)S(1)}, u32[]{:S(2)}, u32[]{:S(2)}) collective-permute-start(bf16[64,4096]{1,0:T(8,128)(2,1)} %bitcast.8), channel_id=1, source_target_pairs={{0,16},{1,17},{2,18},{3,19},{4,20},{5,21},{6,22},{7,23},{8,24},{9,... | collective-permute-start | bytes 1572872 | tf_op jit(solution)/shard_map/ppermute | solution.py:359
  203.9 24.5 %collective-permute-start.2 = (bf16[128,4096]{1,0:T(8,128)(2,1)}, bf16[128,4096]{1,0:T(8,128)(2,1)}, u32[]{:S(2)}, u32[]{:S(2)}) collective-permute-start(bf16[128,4096]{1,0:T(8,128)(2,1)} %pad_maximum_fusion.refs_0_.refs_4_), channel_id=1, source_target_pairs={{0,8},{1,9},{2,10},{3,11},{4,12},{5,13},{6,14},{7,15},{8,0},{9,1},... | collective-permute-start | bytes 3145736 | tf_op jit(solution)/shard_map/ppermute | solution.py:364
  203.9 27.0 %collective-permute-start.3 = (bf16[128,4096]{1,0:T(8,128)(2,1)}, bf16[128,4096]{1,0:T(8,128)(2,1)}, u32[]{:S(2)}, u32[]{:S(2)}) collective-permute-start(bf16[128,4096]{1,0:T(8,128)(2,1)} %pad_maximum_fusion.refs_0_.refs_4_), channel_id=1, source_target_pairs={{0,4},{1,3},{2,6},{3,1},{4,0},{5,7},{6,2},{7,5},{8,12},{9,11},{10,... | collective-permute-start | bytes 3145736 | tf_op jit(solution)/shard_map/ppermute | solution.py:364
  228.4 15.6 %collective-permute-start.4 = (bf16[128,4096]{1,0:T(8,128)(2,1)}, bf16[128,4096]{1,0:T(8,128)(2,1)}, u32[]{:S(2)}, u32[]{:S(2)}) collective-permute-start(bf16[128,4096]{1,0:T(8,128)(2,1)} %collective-permute-done.2.refs_1_.refs_5_), channel_id=1, source_target_pairs={{0,4},{1,3},{2,6},{3,1},{4,0},{5,7},{6,2},{7,5},{8,12},{9,11},{10,... | collective-permute-start | bytes 3145736 | tf_op jit(solution)/shard_map/ppermute | solution.py:364
  248.7 26.4 %collective-permute-start.5 = (bf16[512,2048]{1,0:T(8,128)(2,1)}, bf16[512,2048]{1,0:T(8,128)(2,1)}, u32[]{:S(2)}, u32[]{:S(2)}) collective-permute-start(bf16[512,2048]{1,0:T(8,128)(2,1)} %bitcast.6), channel_id=1, source_target_pairs={{0,2},{1,5},{2,0},{3,7},{4,6},{5,1},{6,4},{7,3},{8,10},{9,13},{10,... | collective-permute-start | bytes 6291464 | tf_op jit(solution)/shard_map/ppermute | solution.py:366
  249.7 25.4 %collective-permute-start.6 = (bf16[512,2048]{1,0:T(8,128)(2,1)}, bf16[512,2048]{1,0:T(8,128)(2,1)}, u32[]{:S(2)}, u32[]{:S(2)}) collective-permute-start(bf16[512,2048]{1,0:T(8,128)(2,1)} %bitcast.10), channel_id=1, source_target_pairs={{0,1},{1,0},{2,3},{3,2},{4,5},{5,4},{6,7},{7,6},{8,9},{9,8},{10,11... | collective-permute-start | bytes 6291464 | tf_op jit(solution)/shard_map/ppermute | solution.py:368
  249.7 46.3 %collective-permute-start.7 = (bf16[512,2048]{1,0:T(8,128)(2,1)}, bf16[512,2048]{1,0:T(8,128)(2,1)}, u32[]{:S(2)}, u32[]{:S(2)}) collective-permute-start(bf16[512,2048]{1,0:T(8,128)(2,1)} %bitcast.11), channel_id=1, source_target_pairs={{0,3},{1,4},{2,1},{3,6},{4,7},{5,0},{6,5},{7,2},{8,11},{9,12},{10,... | collective-permute-start | bytes 6291464 | tf_op jit(solution)/shard_map/ppermute | solution.py:367
  251.4 1.7 copy-start
  258.1 37.9 %collective-permute-start = (bf16[512,1024]{1,0:T(8,128)(2,1)}, bf16[512,1024]{1,0:T(8,128)(2,1)S(1)}, u32[]{:S(2)}, u32[]{:S(2)}) collective-permute-start(bf16[512,1024]{1,0:T(8,128)(2,1)} %combine.1.a_ref), channel_id=1, source_target_pairs={{0,1},{1,0},{2,3},{3,2},{4,5},{5,4},{6,7},{7,6},{8,9},{9,8},{10,11... | collective-permute-start | bytes 3145736 | tf_op jit(solution)/shard_map/ppermute | solution.py:392
  296.1 1.0 copy-start.2
